TPU v7x, 32 devices: a whole 2x2x4 slice. The times are simulated.
32 devices in a mesh: trial: 2 (over core), bank: 4 (over y, x), zero: 4 (over z).
Axes of the slice: x: 2, y: 2, z: 4, core: 2. Of those that a mesh axis runs over, the one named last changes fastest.
Arguments:
- w_gate: float32 [128, 2048, 1024], P(('trial', 'bank'), 'zero'), parts along dimension 0, may hold values from -0.1875 to 0.1875
- w_up: float32 [128, 2048, 1024], P(('trial', 'bank'), 'zero'), parts along dimension 0, may hold values from -0.1875 to 0.1875
- router_weight: float32 [4096, 64], P(('trial', 'zero'), 'bank'), parts along dimension 0, may hold values from -0.125 to 0.125
- router_gain: float32 [4096], P(('trial', 'zero')), parts along dimension 0, may hold values from 0.25 to 1.75
Outputs:
- serve_gate: bfloat16 [128, 2048, 1024], P(('trial', 'bank'), None, 'zero'), parts along dimension 0
- serve_up: bfloat16 [128, 2048, 1024], P(('trial', 'bank'), None, 'zero'), parts along dimension 0
- scale_gate: float32 [128, 1024], P(('trial', 'bank'), 'zero'), parts along dimension 0
- scale_up: float32 [128, 1024], P(('trial', 'bank'), 'zero'), parts along dimension 0
- serve_router: bfloat16 [4096, 64], P('trial'), parts along dimension 0
There are 2 independent parts, one for each index of `trial`. A program takes and returns all parts, laid end to end along the dimension named above; each array names one. Nothing has to cross between parts.
All inputs are finite; a program needn't handle non-finite values. Where the computation divides by a largest or mean magnitude, that divisor is 1e-20 or more.
Results may differ from a plain program's by a relative error of at most 0.001.
Values may be sent and summed in bfloat16 or wider, within the bound.
A program may use at most 192 MiB of HBM per device.

v0:
```python
import functools

import jax
import jax.numpy as jnp
from jax import lax
from jax.experimental import pallas as pl
from jax.experimental.pallas import tpu as pltpu
from jax.sharding import PartitionSpec as P

MESH = pl.DeviceIdType.MESH
SLOTS = 3
STEP = 16
CUTS = 4
HEADS = 2


def plain(n, w_gate, w_up, router_weight, router_gain):
    d_model = w_gate.shape[1] * n

    def rescaled(w):
        scale = lax.psum(jnp.sum(jnp.abs(w), axis=1), "zero") / d_model
        narrow = (w / jnp.expand_dims(scale, 1)).astype(jnp.bfloat16)
        serve = lax.all_to_all(narrow, "zero", split_axis=2, concat_axis=1, tiled=True)
        width = serve.shape[2]
        return serve, lax.dynamic_slice_in_dim(scale, lax.axis_index("zero") * width, width, axis=1)

    serve_gate, scale_gate = rescaled(w_gate)
    serve_up, scale_up = rescaled(w_up)
    part = (router_weight * router_gain[:, None]).astype(jnp.bfloat16)
    row = lax.all_gather(part, "zero", axis=0, tiled=True)
    router = lax.all_gather(row, "bank", axis=1, tiled=True)
    return serve_gate, serve_up, scale_gate, scale_up, router


def kernel(
    n, banks, wg_ref, wu_ref, rw_ref, rg_ref, *refs
):
    og_ref, ou_ref, sg_ref, su_ref, rt_ref = refs[:5]
    tails = refs[5 : 5 + n]
    stage, first, sendbuf, parts, sums, lower, half, across, totals, scales = refs[5 + n : 15 + n]
    (
    tail_sem, in_sem, first_sem, own_sem, send_sem, recv_sem, x_send, x_recv, up_send, up_recv, mid_send, mid_recv,
    down_send, down_recv, rz_send, rz_recv, rb_send, rb_recv,
    ) = refs[15 + n :]
    me = lax.axis_index("zero")
    bank = lax.axis_index("bank")
    lead = lax.rem(lax.axis_index("trial"), 2) == 0
    w, o, so = (wg_ref, wu_ref), (og_ref, ou_ref), (sg_ref, su_ref)
    experts, rows, cols = wg_ref.shape
    width = cols // n
    d_model = rows * n
    last = experts - 1
    piece = rows // CUTS
    heads = [(m, e) for e in range(HEADS) for m in range(2)]

    def head(m, e, c):
        at = pl.ds(c * piece, piece)
        return pltpu.make_async_copy(w[m].at[e, at], first.at[m, e, at], first_sem.at[m, e, c])

    def load(m, e, slot):
        return pltpu.make_async_copy(w[m].at[e], stage.at[m, slot], in_sem.at[m, slot])

    def refill():
        for e in range(HEADS, min(HEADS + SLOTS, experts)):
            for m in range(2):
                load(m, e, e % SLOTS).start()

    for m, e in heads[:2]:
        for c in range(CUTS):
            head(m, e, c).start()

    def others(axis, here, count, act):
        for p in range(count):
            @pl.when(here != p)
            def _():
                act(p)

    barrier = pltpu.get_barrier_semaphore()

    def greet(axis):
        return lambda p: pl.semaphore_signal(barrier, inc=1, device_id={axis: p}, device_id_type=MESH)

    others("zero", me, n, greet("zero"))
    others("bank", bank, banks, greet("bank"))

    def sizes_of(src, count, acc):
        def body(r, acc):
            return acc + jnp.abs(src[pl.ds(pl.multiple_of(r * 8, 8), 8), :])

        return lax.fori_loop(0, count // 8, body, acc, unroll=8)

    empty = jnp.zeros((8, cols), jnp.float32)

    def head_sizes(m, e):
        acc = empty
        for c in range(CUTS):
            head(m, e, c).wait()
            acc = sizes_of(first.at[m, e, pl.ds(c * piece, piece)], piece, acc)
        parts[me, e, m] = jnp.sum(acc, axis=0, keepdims=True)

    def swap(m, e, s, p):
        return pltpu.make_async_remote_copy(
            src_ref=parts.at[s, e, m], dst_ref=parts.at[s, e, m],
            send_sem=x_send.at[m, e, p], recv_sem=x_recv.at[m, e, s],
            device_id={"zero": p}, device_id_type=MESH,
        )

    def arrived(m, e):
        others("zero", me, n, lambda p: swap(m, e, p, p).wait_recv())
        total = parts[0, e, m]
        for s in range(1, n):
            total = total + parts[s, e, m]
        totals[e, m] = total

    def narrow(src, m, e):
        scale = totals[e, m] / d_model
        factor = 1.0 / scale
        scales[...] = scale
        so[m][pl.ds(e, 1), :] = scales[:, pl.ds(pl.multiple_of(me * width, width), width)]

        def body(r, carry):
            at = pl.ds(pl.multiple_of(r * STEP, STEP), STEP)
            for c in range(n):
                lanes = slice(c * width, (c + 1) * width)
                sendbuf[m, e, c, at, :] = (src[at, lanes] * factor[:, lanes]).astype(jnp.bfloat16)
            return carry

        lax.fori_loop(0, rows // STEP, body, 0, unroll=2)

    def place(ref, e, s):
        return ref.at[e, pl.ds(pl.multiple_of(s * rows, rows), rows), :]

    def keep(m, e):
        pltpu.make_async_copy(sendbuf.at[m, e, me], place(o[m], e, me), own_sem.at[m]).start()

    def send(m, e, p):
        pltpu.make_async_remote_copy(
            src_ref=sendbuf.at[m, e, p], dst_ref=place(o[m], e, me),
            send_sem=send_sem.at[m, p], recv_sem=recv_sem.at[m, me],
            device_id={"zero": p}, device_id_type=MESH,
        ).start()

    def send_at(m, e, t):
        @pl.when(me + t < n)
        def _():
            send(m, e, me + t)

        @pl.when(me - t >= 0)
        def _():
            send(m, e, me - t)

    def send_all(m, e):
        for t in range(n - 1, 0, -1):
            send_at(m, e, t)

    for i, (m, e) in enumerate(heads):
        head_sizes(m, e)
        if i == 0:
            for later in heads[2:]:
                for c in range(CUTS):
                    head(*later, c).start()
            pl.semaphore_wait(barrier, n - 1 + banks - 1)
        others("zero", me, n, lambda p: swap(m, e, me, p).start())
        if i == 1:
            refill()

            @pl.when(lead)
            def _():
                for k in heads[:2]:
                    arrived(*k)
                    narrow(first.at[k], *k)
                    send_all(*k)
                    keep(*k)

    @pl.when(lead)
    def _():
        for k in heads[2:]:
            arrived(*k)
            narrow(first.at[k], *k)
            send_all(*k)
            keep(*k)

    depth = rw_ref.shape[1]
    mine = pl.ds(pl.multiple_of(me * depth, depth), depth)
    rt_ref[bank, :, mine] = (rw_ref[...] * rg_ref[...]).astype(jnp.bfloat16)

    def sizes(e, carry):
        slot = lax.rem(e, SLOTS)
        for m in range(2):
            load(m, e, slot).wait()
            acc = sizes_of(stage.at[m, slot], rows, empty)
            sums[e, m] = jnp.sum(acc, axis=0, keepdims=True)

            @pl.when(e + SLOTS < experts)
            def _():
                load(m, e + SLOTS, slot).start()
        return carry

    lax.fori_loop(HEADS, experts, sizes, 0)
    refill()

    span = pl.ds(HEADS, experts - HEADS)
    gates = (n // 2 - 1, n // 2)

    def members(g):
        side = range(n // 2) if g < n // 2 else range(n // 2, n)
        return [(i, p) for i, p in enumerate(p for p in side if p != g)]

    def rise(g, i):
        return pltpu.make_async_remote_copy(
            src_ref=sums.at[span], dst_ref=lower.at[i, span], send_sem=up_send, recv_sem=up_recv.at[i],
            device_id={"zero": g}, device_id_type=MESH,
        )

    def meet(g):
        return pltpu.make_async_remote_copy(
            src_ref=half.at[span], dst_ref=across.at[span], send_sem=mid_send, recv_sem=mid_recv,
            device_id={"zero": n - 1 - g}, device_id_type=MESH,
        )

    def give(i, p):
        return pltpu.make_async_remote_copy(
            src_ref=totals.at[span], dst_ref=totals.at[span], send_sem=down_send.at[i], recv_sem=down_recv,
            device_id={"zero": p}, device_id_type=MESH,
        )

    for g in gates:
        for i, p in members(g):
            @pl.when(me == p)
            def _():
                rise(g, i).start()

    @pl.when(jnp.logical_not(lead))
    def _():
        for k in heads:
            arrived(*k)
            narrow(first.at[k], *k)

    for g in gates:
        @pl.when(me == g)
        def _():
            total = sums[span]
            for i, p in members(g):
                rise(g, i).wait_recv()
                total = total + lower[i, span]
            half[span] = total
            meet(g).start()
            meet(g).wait_recv()
            totals[span] = half[span] + across[span]
            for i, p in members(g):
                give(i, p).start()

        for i, p in members(g):
            @pl.when(me == p)
            def _():
                give(i, p).wait_recv()

    def row_copy(s, p):
        at = pl.ds(pl.multiple_of(s * depth, depth), depth)
        return pltpu.make_async_remote_copy(
            src_ref=rt_ref.at[bank, :, at], dst_ref=rt_ref.at[bank, :, at],
            send_sem=rz_send.at[p], recv_sem=rz_recv.at[s],
            device_id={"zero": p}, device_id_type=MESH,
        )

    others("zero", me, n, lambda p: row_copy(me, p).start())

    @pl.when(jnp.logical_not(lead))
    def _():
        for k in heads:
            send_all(*k)
            keep(*k)

    def put(m, d):
        return pltpu.make_async_copy(
            sendbuf.at[m, last, lax.rem(me + d, n)], tails[d].at[m], tail_sem.at[d, m]
        )

    def narrowed(e, carry):
        slot = lax.rem(e, SLOTS)
        for m in range(2):
            load(m, e, slot).wait()
            narrow(stage.at[m, slot], m, e)

            @pl.when(e + SLOTS < experts)
            def _():
                load(m, e + SLOTS, slot).start()

            @pl.when(e < last)
            def _():
                send_at(m, e, 1)
                keep(m, e)
        return carry

    lax.fori_loop(HEADS, experts, narrowed, 0)
    for m in range(2):
        for d in range(n):
            put(m, d).start()

    def far(e, carry):
        for m in range(2):
            for t in range(2, n):
                send_at(m, e, t)
        return carry

    lax.fori_loop(HEADS, last, far, 0)
    for m in range(2):
        for d in range(n):
            put(m, d).wait()

    others("zero", me, n, lambda p: row_copy(p, p).wait_recv())

    def column_copy(s, p):
        return pltpu.make_async_remote_copy(
            src_ref=rt_ref.at[s], dst_ref=rt_ref.at[s],
            send_sem=rb_send.at[p], recv_sem=rb_recv.at[s],
            device_id={"bank": p}, device_id_type=MESH,
        )

    others("bank", bank, banks, lambda p: column_copy(bank, p).start())
    others("bank", bank, banks, lambda p: column_copy(p, p).wait_recv())
    others("bank", bank, banks, lambda p: column_copy(bank, p).wait_send())
    others("zero", me, n, lambda p: row_copy(me, p).wait_send())
    for m, e in heads:
        others("zero", me, n, lambda p: swap(m, e, me, p).wait_send())
    for g in gates:
        @pl.when(me == g)
        def _():
            meet(g).wait_send()
            for i, p in members(g):
                give(i, p).wait_send()

        for i, p in members(g):
            @pl.when(me == p)
            def _():
                rise(g, i).wait_send()

    for m in range(2):
        def whole(s, p):
            return pltpu.make_async_remote_copy(
                src_ref=sendbuf.at[m, pl.ds(0, last), p],
                dst_ref=o[m].at[:, pl.ds(pl.multiple_of(s * rows, rows), rows), :],
                send_sem=send_sem.at[m, p], recv_sem=recv_sem.at[m, s],
                device_id={"zero": p}, device_id_type=MESH,
            )

        pltpu.make_async_copy(
            sendbuf.at[m, pl.ds(0, last), me], o[m].at[:, pl.ds(pl.multiple_of(me * rows, rows), rows), :], own_sem.at[m]
        ).wait()
        others("zero", me, n, lambda p: whole(me, p).wait_send())
        others("zero", me, n, lambda p: whole(p, p).wait_recv())


def copy_kernel(n, a_ref, b_ref, own_ref, sa_ref, sb_ref, rt_ref, *outs):
    c_ref, d_ref = outs[:2]
    e = pl.program_id(0)
    rows = own_ref.shape[1]

    @pl.when(e < pl.num_programs(0) - 1)
    def _():
        c_ref[...] = a_ref[...]
        d_ref[...] = b_ref[...]

    @pl.when(e == 0)
    def _():
        for src, dst in zip((sa_ref, sb_ref, rt_ref), outs[2:]):
            dst[...] = src[...]

    @pl.when(e == pl.num_programs(0) - 1)
    def _():
        at = pl.ds(pl.multiple_of(lax.axis_index("zero") * rows, rows), rows)
        c_ref[0, at, :] = own_ref[0]
        d_ref[0, at, :] = own_ref[1]


def spread(n, og, ou, own, *small):
    main, height, width = og.shape
    block = pl.BlockSpec((1, height, width), lambda e: (e, 0, 0))
    front = pl.BlockSpec((1, height, width), lambda e: (jnp.minimum(e, main - 1), 0, 0))
    out = jax.ShapeDtypeStruct((main + 1, height, width), og.dtype)

    def all_of(a):
        return pl.BlockSpec(a.shape, lambda e: (0,) * a.ndim)

    return pl.pallas_call(
        functools.partial(copy_kernel, n),
        grid=(main + 1,),
        in_specs=[front, front] + [all_of(a) for a in (own, *small)],
        out_specs=(block, block, *[all_of(a) for a in small]),
        out_shape=(out, out, *[jax.ShapeDtypeStruct(a.shape, a.dtype) for a in small]),
        cost_estimate=pl.CostEstimate(flops=0, bytes_accessed=8 * og.size, transcendentals=0),
        name="spread",
    )(og, ou, own, *small)


def join_kernel(n, shifts, *refs):
    count = len(shifts)
    blocks, outs, sem = refs[2 : 2 + count], refs[2 + count : 4 + count], refs[4 + count]
    me = lax.axis_index("zero")
    last = outs[0].shape[0] - 1
    rows = blocks[0].shape[1]
    copies = []
    for i, d in enumerate(shifts):
        at = pl.ds(pl.multiple_of(lax.rem(me - d + n, n) * rows, rows), rows)
        for m in range(2):
            copies.append(pltpu.make_async_copy(blocks[i].at[m], outs[m].at[last, at, :], sem.at[i, m]))
    for copy in copies:
        copy.start()
    for copy in copies:
        copy.wait()


def join(n, shifts, og, ou, blocks):
    anywhere = pl.BlockSpec(memory_space=pl.ANY)
    vmem = pl.BlockSpec(memory_space=pltpu.VMEM)
    return pl.pallas_call(
        functools.partial(join_kernel, n, shifts),
        out_shape=(jax.ShapeDtypeStruct(og.shape, og.dtype), jax.ShapeDtypeStruct(ou.shape, ou.dtype)),
        in_specs=[anywhere, anywhere] + [vmem] * len(blocks),
        out_specs=(anywhere, anywhere),
        scratch_shapes=[pltpu.SemaphoreType.DMA((len(blocks), 2))],
        input_output_aliases={0: 0, 1: 1},
        compiler_params=pltpu.CompilerParams(vmem_limit_bytes=8 * 1024 * 1024),
        name="join",
    )(og, ou, *blocks)


def local(n, banks, w_gate, w_up, router_weight, router_gain):
    experts, rows, cols = w_gate.shape
    width = cols // n
    depth, heads = router_weight.shape
    fits = width % 128 == 0 and rows % (8 * CUTS) == 0 and depth % 128 == 0 and heads % 16 == 0
    fits = fits and experts > HEADS + 1 and n % 2 == 0
    if not fits:
        return plain(n, w_gate, w_up, router_weight, router_gain)
    anywhere = pl.BlockSpec(memory_space=pl.ANY)
    vmem = pl.BlockSpec(memory_space=pltpu.VMEM)
    dma = pltpu.SemaphoreType.DMA
    serve = jax.ShapeDtypeStruct((experts - 1, rows * n, width), jnp.bfloat16)
    tail = jax.ShapeDtypeStruct((2, rows, width), jnp.bfloat16)
    scale = jax.ShapeDtypeStruct((experts, width), jnp.float32)
    sizes = pltpu.VMEM((experts, 2, 1, cols), jnp.float32)
    og, ou, sg, su, rt, *tails = pl.pallas_call(
        functools.partial(kernel, n, banks),
        out_shape=(serve, serve, scale, scale, jax.ShapeDtypeStruct((banks, heads, depth * n), jnp.bfloat16), *[tail] * n),
        in_specs=[anywhere, anywhere, vmem, vmem],
        out_specs=(anywhere, anywhere, vmem, vmem, vmem, *[anywhere] * n),
        scratch_shapes=[
            pltpu.VMEM((2, SLOTS, rows, cols), jnp.float32),
            pltpu.VMEM((2, HEADS, rows, cols), jnp.float32),
            pltpu.VMEM((2, experts, n, rows, width), jnp.bfloat16),
            pltpu.VMEM((n, HEADS, 2, 1, cols), jnp.float32),
            sizes,
            pltpu.VMEM((max(n // 2 - 1, 1), experts, 2, 1, cols), jnp.float32),
            sizes, sizes, sizes,
            pltpu.VMEM((1, cols), jnp.float32),
            dma((n, 2)), dma((2, SLOTS)), dma((2, HEADS, CUTS)), dma((2,)), dma((2, n)), dma((2, n)),
            dma((2, HEADS, n)), dma((2, HEADS, n)), dma, dma((n,)), dma, dma, dma((n,)), dma,
            dma((n,)), dma((n,)), dma((banks,)), dma((banks,)),
        ],
        compiler_params=pltpu.CompilerParams(
            collective_id=0, has_side_effects=True, vmem_limit_bytes=58 * 1024 * 1024
        ),
    )(w_gate, w_up, router_weight.T, router_gain[None, :])
    arrived = [
        lax.ppermute(tails[d], "zero", [(i, (i + d) % n) for i in range(n)]) for d in range(1, n)
    ]
    og, ou, sg, su, rt = spread(n, og, ou, tails[0], sg, su, rt)
    if n > 2:
        og, ou = join(n, tuple(range(1, n - 1)), og, ou, arrived[:-1])
    og, ou = join(n, (n - 1,), og, ou, arrived[-1:])
    return og, ou, sg, su, rt.reshape(banks * heads, depth * n).T


def solution(mesh):
    n, banks = mesh.shape["zero"], mesh.shape["bank"]
    return jax.shard_map(
        functools.partial(local, n, banks),
        mesh=mesh,
        in_specs=(
            P(("trial", "bank"), "zero", None),
            P(("trial", "bank"), "zero", None),
            P(("trial", "zero"), "bank"),
            P(("trial", "zero")),
        ),
        out_specs=(
            P(("trial", "bank"), None, "zero"),
            P(("trial", "bank"), None, "zero"),
            P(("trial", "bank"), "zero"),
            P(("trial", "bank"), "zero"),
            P("trial", None),
        ),
        check_vma=False,
    )
```

profile of v0, /device:TPU:8, one launch (start us, length us, event | category | flops | bytes accessed | tf_op | source)
XLA Modules:
  0.0 737.3 jit_solution(530983974045177295)
XLA Ops:
  0.6 683.2 %shard_map.83 = (bf16[15,2048,256]{2,1,0:T(8,128)(2,1)}, bf16[15,2048,256]{2,1,0:T(8,128)(2,1)}, f32[16,256]{1,0:T(8,128)}, f32[16,256]{1,0:T(8,128)}, bf16[4,16...) custom-call(f32[16,512,1024]{2,1,0:T(8,128)} %wg_ref.1, ...), custom_call_target="tpu_custom_call" | custom-call | tf_op jit(solution)/shard_map/pallas_call | solution.py:443
  683.8 3.3 collective-permute-start
  687.1 4.4 collective-permute-start.1
  691.5 0.0 collective-permute-start.2
  691.5 27.3 %spread.1 = (bf16[16,2048,256]{2,1,0:T(8,128)(2,1)}, bf16[16,2048,256]{2,1,0:T(8,128)(2,1)}, f32[16,256]{1,0:T(8,128)}, f32[16,256]{1,0:T(8,128)}, bf16[4,16,2048]{2,1,0:T(8,128)(2,1)}) custom-call(bf16[15,2048,256]{2,1,0:T(8,128)(2,1)} %get-tuple-element.23.a_ref, bf16[15,2048,256]{2,1,0:T(8,128)(2,1)} %get-tuple-element.24.b_ref, ...), custom_call_target="tpu_custom_call" | custom-call | bytes 62914560 | tf_op jit(solution)/shard_map/spread/pallas_call | solution.py:385
  718.8 0.0 collective-permute-done.refs_2_
  718.8 12.3 %collective-permute-done.1.refs_3_ = bf16[2,512,256]{2,1,0:T(8,128)(2,1)S(1)} collective-permute-done((bf16[2,512,256]{2,1,0:T(8,128)(2,1)}, bf16[2,512,256]{2,1,0:T(8,128)(2,1)S(1)}, u32[]{:S(2)}, u32[]{:S(2)}) %collective-permute-start.1) | collective-permute-done | bytes 524320 | tf_op jit(solution)/shard_map/ppermute | solution.py:466
  731.1 1.0 join.2
  732.1 4.4 collective-permute-done.2.refs_2_
  736.5 0.8 join.3
Async XLA Ops:
  683.8 35.0 %collective-permute-start = (bf16[2,512,256]{2,1,0:T(8,128)(2,1)}, bf16[2,512,256]{2,1,0:T(8,128)(2,1)S(1)}, u32[]{:S(2)}, u32[]{:S(2)}) collective-permute-start(bf16[2,512,256]{2,1,0:T(8,128)(2,1)} %get-tuple-element.31), channel_id=1, source_target_pairs={{0,1},{1,2},{2,3},{3,0},{4,5},{5,6},{6,7},{7,4},{8,9},{9,10},{10,1... | collective-permute-start | bytes 1572872 | tf_op jit(solution)/shard_map/ppermute | solution.py:466
  687.1 44.0 %collective-permute-start.1 = (bf16[2,512,256]{2,1,0:T(8,128)(2,1)}, bf16[2,512,256]{2,1,0:T(8,128)(2,1)S(1)}, u32[]{:S(2)}, u32[]{:S(2)}) collective-permute-start(bf16[2,512,256]{2,1,0:T(8,128)(2,1)} %get-tuple-element.32), channel_id=1, source_target_pairs={{0,2},{1,3},{2,0},{3,1},{4,6},{5,7},{6,4},{7,5},{8,10},{9,11},{10,... | collective-permute-start | bytes 1572872 | tf_op jit(solution)/shard_map/ppermute | solution.py:466
  691.5 45.0 %collective-permute-start.2 = (bf16[2,512,256]{2,1,0:T(8,128)(2,1)}, bf16[2,512,256]{2,1,0:T(8,128)(2,1)S(1)}, u32[]{:S(2)}, u32[]{:S(2)}) collective-permute-start(bf16[2,512,256]{2,1,0:T(8,128)(2,1)} %get-tuple-element.35), channel_id=1, source_target_pairs={{0,3},{1,0},{2,1},{3,2},{4,7},{5,4},{6,5},{7,6},{8,11},{9,8},{10,9... | collective-permute-start | bytes 1572872 | tf_op jit(solution)/shard_map/ppermute | solution.py:466
where the time goes:
time: 739 us; the launch traced here: 737 us
  Pallas kernels  712 us (96%)
  waiting for transfers between devices  16.7 us (2%)
  starting transfers between devices  7.67 us (1%)
    pallas_call x1, Pallas kernels, local(): pl.pallas_call(functools.partial(kernel, n, banks), out_shape=(serve, ser...  683 us
    pallas_call x1, Pallas kernels, spread(): pl.pallas_call(functools.partial(copy_kernel, n), grid=(main + 1,), in_sp...  27.3 us
    ppermute x3, waiting for transfers between devices, local(): lax.ppermute(tails[d], 'zero', [(i, (i + d) % n) for i in range(n)])  16.7 us
  transfers between devices with their start and end apart: 3, of which 2 were waited for; matrix products, arithmetic and copies ran while one was open for 0% of the time, Pallas kernels for 4%

commit v1 on v0

--- a/solution.py
+++ b/solution.py
@@ -12,6 +12,7 @@
 STEP = 16
 CUTS = 4
 HEADS = 2
+TAIL = 2
 
 
 def plain(n, w_gate, w_up, router_weight, router_gain):
@@ -37,19 +38,19 @@
 ):
     og_ref, ou_ref, sg_ref, su_ref, rt_ref = refs[:5]
     tails = refs[5 : 5 + n]
-    stage, first, sendbuf, parts, sums, lower, half, across, totals, scales = refs[5 + n : 15 + n]
+    stage, first, sendbuf, parts, sums, lower, half, across, totals, scales, router, gain = refs[5 + n : 17 + n]
     (
     tail_sem, in_sem, first_sem, own_sem, send_sem, recv_sem, x_send, x_recv, up_send, up_recv, mid_send, mid_recv,
-    down_send, down_recv, rz_send, rz_recv, rb_send, rb_recv,
-    ) = refs[15 + n :]
+    down_send, down_recv, rz_send, rz_recv, rb_send, rb_recv, r_sem,
+    ) = refs[17 + n :]
     me = lax.axis_index("zero")
     bank = lax.axis_index("bank")
-    lead = lax.rem(lax.axis_index("trial"), 2) == 0
+    lead = lax.rem(lax.axis_index("trial"), 2) == 1
     w, o, so = (wg_ref, wu_ref), (og_ref, ou_ref), (sg_ref, su_ref)
     experts, rows, cols = wg_ref.shape
     width = cols // n
     d_model = rows * n
-    last = experts - 1
+    main = experts - TAIL
     piece = rows // CUTS
     heads = [(m, e) for e in range(HEADS) for m in range(2)]
 
@@ -68,6 +69,9 @@
     for m, e in heads[:2]:
         for c in range(CUTS):
             head(m, e, c).start()
+    small = [pltpu.make_async_copy(src, dst, r_sem.at[i]) for i, (src, dst) in enumerate(((rw_ref, router), (rg_ref, gain)))]
+    for copy in small:
+        copy.start()
 
     def others(axis, here, count, act):
         for p in range(count):
@@ -152,6 +156,20 @@
     def send_all(m, e):
         for t in range(n - 1, 0, -1):
             send_at(m, e, t)
+
+    depth = rw_ref.shape[1]
+    mine = pl.ds(pl.multiple_of(me * depth, depth), depth)
+    for copy in small:
+        copy.wait()
+    rt_ref[bank, :, mine] = (router[...] * gain[...]).astype(jnp.bfloat16)
+
+    def row_copy(s, p):
+        at = pl.ds(pl.multiple_of(s * depth, depth), depth)
+        return pltpu.make_async_remote_copy(
+            src_ref=rt_ref.at[bank, :, at], dst_ref=rt_ref.at[bank, :, at],
+            send_sem=rz_send.at[p], recv_sem=rz_recv.at[s],
+            device_id={"zero": p}, device_id_type=MESH,
+        )
 
     for i, (m, e) in enumerate(heads):
         head_sizes(m, e)
@@ -162,6 +180,7 @@
             pl.semaphore_wait(barrier, n - 1 + banks - 1)
         others("zero", me, n, lambda p: swap(m, e, me, p).start())
         if i == 1:
+            others("zero", me, n, lambda p: row_copy(me, p).start())
             refill()
 
             @pl.when(lead)
@@ -179,10 +198,6 @@
             narrow(first.at[k], *k)
             send_all(*k)
             keep(*k)
-
-    depth = rw_ref.shape[1]
-    mine = pl.ds(pl.multiple_of(me * depth, depth), depth)
-    rt_ref[bank, :, mine] = (rw_ref[...] * rg_ref[...]).astype(jnp.bfloat16)
 
     def sizes(e, carry):
         slot = lax.rem(e, SLOTS)
@@ -255,15 +270,34 @@
             def _():
                 give(i, p).wait_recv()
 
-    def row_copy(s, p):
-        at = pl.ds(pl.multiple_of(s * depth, depth), depth)
-        return pltpu.make_async_remote_copy(
-            src_ref=rt_ref.at[bank, :, at], dst_ref=rt_ref.at[bank, :, at],
-            send_sem=rz_send.at[p], recv_sem=rz_recv.at[s],
-            device_id={"zero": p}, device_id_type=MESH,
-        )
-
-    others("zero", me, n, lambda p: row_copy(me, p).start())
+    def put(m, d):
+        return pltpu.make_async_copy(
+            sendbuf.at[m, pl.ds(main, TAIL), lax.rem(me + d, n)], tails[d].at[m], tail_sem.at[d, m]
+        )
+
+    def narrowed(e, carry):
+        slot = lax.rem(e, SLOTS)
+        for m in range(2):
+            load(m, e, slot).wait()
+            narrow(stage.at[m, slot], m, e)
+
+            @pl.when(e + SLOTS < experts)
+            def _():
+                load(m, e + SLOTS, slot).start()
+
+            @pl.when(e < main)
+            def _():
+                keep(m, e)
+
+                @pl.when(lead)
+                def _():
+                    send_at(m, e, 1)
+        return carry
+
+    lax.fori_loop(HEADS, experts, narrowed, 0)
+    for m in range(2):
+        for d in range(n):
+            put(m, d).start()
 
     @pl.when(jnp.logical_not(lead))
     def _():
@@ -271,31 +305,12 @@
             send_all(*k)
             keep(*k)
 
-    def put(m, d):
-        return pltpu.make_async_copy(
-            sendbuf.at[m, last, lax.rem(me + d, n)], tails[d].at[m], tail_sem.at[d, m]
-        )
-
-    def narrowed(e, carry):
-        slot = lax.rem(e, SLOTS)
-        for m in range(2):
-            load(m, e, slot).wait()
-            narrow(stage.at[m, slot], m, e)
-
-            @pl.when(e + SLOTS < experts)
-            def _():
-                load(m, e + SLOTS, slot).start()
-
-            @pl.when(e < last)
-            def _():
+        def near(e, carry):
+            for m in range(2):
                 send_at(m, e, 1)
-                keep(m, e)
-        return carry
-
-    lax.fori_loop(HEADS, experts, narrowed, 0)
-    for m in range(2):
-        for d in range(n):
-            put(m, d).start()
+            return carry
+
+        lax.fori_loop(HEADS, main, near, 0)
 
     def far(e, carry):
         for m in range(2):
@@ -303,7 +318,7 @@
                 send_at(m, e, t)
         return carry
 
-    lax.fori_loop(HEADS, last, far, 0)
+    lax.fori_loop(HEADS, main, far, 0)
     for m in range(2):
         for d in range(n):
             put(m, d).wait()
@@ -338,14 +353,14 @@
     for m in range(2):
         def whole(s, p):
             return pltpu.make_async_remote_copy(
-                src_ref=sendbuf.at[m, pl.ds(0, last), p],
+                src_ref=sendbuf.at[m, pl.ds(0, main), p],
                 dst_ref=o[m].at[:, pl.ds(pl.multiple_of(s * rows, rows), rows), :],
                 send_sem=send_sem.at[m, p], recv_sem=recv_sem.at[m, s],
                 device_id={"zero": p}, device_id_type=MESH,
             )
 
         pltpu.make_async_copy(
-            sendbuf.at[m, pl.ds(0, last), me], o[m].at[:, pl.ds(pl.multiple_of(me * rows, rows), rows), :], own_sem.at[m]
+            sendbuf.at[m, pl.ds(0, main), me], o[m].at[:, pl.ds(pl.multiple_of(me * rows, rows), rows), :], own_sem.at[m]
         ).wait()
         others("zero", me, n, lambda p: whole(me, p).wait_send())
         others("zero", me, n, lambda p: whole(p, p).wait_recv())
@@ -354,9 +369,10 @@
 def copy_kernel(n, a_ref, b_ref, own_ref, sa_ref, sb_ref, rt_ref, *outs):
     c_ref, d_ref = outs[:2]
     e = pl.program_id(0)
-    rows = own_ref.shape[1]
-
-    @pl.when(e < pl.num_programs(0) - 1)
+    tail, rows = own_ref.shape[1:3]
+    main = pl.num_programs(0) - tail
+
+    @pl.when(e < main)
     def _():
         c_ref[...] = a_ref[...]
         d_ref[...] = b_ref[...]
@@ -366,25 +382,26 @@
         for src, dst in zip((sa_ref, sb_ref, rt_ref), outs[2:]):
             dst[...] = src[...]
 
-    @pl.when(e == pl.num_programs(0) - 1)
+    @pl.when(e >= main)
     def _():
         at = pl.ds(pl.multiple_of(lax.axis_index("zero") * rows, rows), rows)
-        c_ref[0, at, :] = own_ref[0]
-        d_ref[0, at, :] = own_ref[1]
+        c_ref[0, at, :] = own_ref[0, e - main]
+        d_ref[0, at, :] = own_ref[1, e - main]
 
 
 def spread(n, og, ou, own, *small):
     main, height, width = og.shape
     block = pl.BlockSpec((1, height, width), lambda e: (e, 0, 0))
     front = pl.BlockSpec((1, height, width), lambda e: (jnp.minimum(e, main - 1), 0, 0))
-    out = jax.ShapeDtypeStruct((main + 1, height, width), og.dtype)
+    experts = main + own.shape[1]
+    out = jax.ShapeDtypeStruct((experts, height, width), og.dtype)
 
     def all_of(a):
         return pl.BlockSpec(a.shape, lambda e: (0,) * a.ndim)
 
     return pl.pallas_call(
         functools.partial(copy_kernel, n),
-        grid=(main + 1,),
+        grid=(experts,),
         in_specs=[front, front] + [all_of(a) for a in (own, *small)],
         out_specs=(block, block, *[all_of(a) for a in small]),
         out_shape=(out, out, *[jax.ShapeDtypeStruct(a.shape, a.dtype) for a in small]),
@@ -397,13 +414,13 @@
     count = len(shifts)
     blocks, outs, sem = refs[2 : 2 + count], refs[2 + count : 4 + count], refs[4 + count]
     me = lax.axis_index("zero")
-    last = outs[0].shape[0] - 1
-    rows = blocks[0].shape[1]
+    tail, rows = blocks[0].shape[1:3]
+    ends = pl.ds(outs[0].shape[0] - tail, tail)
     copies = []
     for i, d in enumerate(shifts):
         at = pl.ds(pl.multiple_of(lax.rem(me - d + n, n) * rows, rows), rows)
         for m in range(2):
-            copies.append(pltpu.make_async_copy(blocks[i].at[m], outs[m].at[last, at, :], sem.at[i, m]))
+            copies.append(pltpu.make_async_copy(blocks[i].at[m], outs[m].at[ends, at, :], sem.at[i, m]))
     for copy in copies:
         copy.start()
     for copy in copies:
@@ -430,20 +447,20 @@
     width = cols // n
     depth, heads = router_weight.shape
     fits = width % 128 == 0 and rows % (8 * CUTS) == 0 and depth % 128 == 0 and heads % 16 == 0
-    fits = fits and experts > HEADS + 1 and n % 2 == 0
+    fits = fits and experts > HEADS + TAIL and n % 2 == 0
     if not fits:
         return plain(n, w_gate, w_up, router_weight, router_gain)
     anywhere = pl.BlockSpec(memory_space=pl.ANY)
     vmem = pl.BlockSpec(memory_space=pltpu.VMEM)
     dma = pltpu.SemaphoreType.DMA
-    serve = jax.ShapeDtypeStruct((experts - 1, rows * n, width), jnp.bfloat16)
-    tail = jax.ShapeDtypeStruct((2, rows, width), jnp.bfloat16)
+    serve = jax.ShapeDtypeStruct((experts - TAIL, rows * n, width), jnp.bfloat16)
+    tail = jax.ShapeDtypeStruct((2, TAIL, rows, width), jnp.bfloat16)
     scale = jax.ShapeDtypeStruct((experts, width), jnp.float32)
     sizes = pltpu.VMEM((experts, 2, 1, cols), jnp.float32)
     og, ou, sg, su, rt, *tails = pl.pallas_call(
         functools.partial(kernel, n, banks),
         out_shape=(serve, serve, scale, scale, jax.ShapeDtypeStruct((banks, heads, depth * n), jnp.bfloat16), *[tail] * n),
-        in_specs=[anywhere, anywhere, vmem, vmem],
+        in_specs=[anywhere] * 4,
         out_specs=(anywhere, anywhere, vmem, vmem, vmem, *[anywhere] * n),
         scratch_shapes=[
             pltpu.VMEM((2, SLOTS, rows, cols), jnp.float32),
@@ -454,9 +471,11 @@
             pltpu.VMEM((max(n // 2 - 1, 1), experts, 2, 1, cols), jnp.float32),
             sizes, sizes, sizes,
             pltpu.VMEM((1, cols), jnp.float32),
+            pltpu.VMEM((heads, depth), jnp.float32),
+            pltpu.VMEM((1, depth), jnp.float32),
             dma((n, 2)), dma((2, SLOTS)), dma((2, HEADS, CUTS)), dma((2,)), dma((2, n)), dma((2, n)),
             dma((2, HEADS, n)), dma((2, HEADS, n)), dma, dma((n,)), dma, dma, dma((n,)), dma,
-            dma((n,)), dma((n,)), dma((banks,)), dma((banks,)),
+            dma((n,)), dma((n,)), dma((banks,)), dma((banks,)), dma((2,)),
         ],
         compiler_params=pltpu.CompilerParams(
             collective_id=0, has_side_effects=True, vmem_limit_bytes=58 * 1024 * 1024

time: 739 us -> 734 us (level)
  Pallas kernels: 712 us -> 703 us
    pallas_call x1, Pallas kernels: 683 us -> 675 us  [local(): pl.pallas_call(functools.partial(kernel, n, banks), out_shape=(serve, ser...]
where the time goes in v1:
time: 734 us; the launch traced here: 733 us
  Pallas kernels  703 us (96%)
  waiting for transfers between devices  24 us (3%)
    pallas_call x1, Pallas kernels, local(): pl.pallas_call(functools.partial(kernel, n, banks), out_shape=(serve, ser...  675 us
    pallas_call x1, Pallas kernels, spread(): pl.pallas_call(functools.partial(copy_kernel, n), grid=(experts,), in_spe...  25.4 us
    ppermute x3, waiting for transfers between devices, local(): lax.ppermute(tails[d], 'zero', [(i, (i + d) % n) for i in range(n)])  24 us
  transfers between devices with their start and end apart: 3, of which 2 were waited for; matrix products, arithmetic and copies ran while one was open for 0% of the time, Pallas kernels for 4%

profile of v1, /device:TPU:8, one launch (start us, length us, event | category | flops | bytes accessed | tf_op | source)
XLA Modules:
  0.0 733.4 jit_solution(1771936384772923051)
XLA Ops:
  0.6 675.5 %shard_map.83 = (bf16[14,2048,256]{2,1,0:T(8,128)(2,1)}, bf16[14,2048,256]{2,1,0:T(8,128)(2,1)}, f32[16,256]{1,0:T(8,128)}, f32[16,256]{1,0:T(8,128)}, bf16[4,16...) custom-call(f32[16,512,1024]{2,1,0:T(8,128)} %wg_ref.1, ...), custom_call_target="tpu_custom_call" | custom-call | tf_op jit(solution)/shard_map/pallas_call | solution.py:460
  676.1 0.1 collective-permute-start
  676.2 3.5 collective-permute-start.1
  679.7 1.9 collective-permute-start.2
  681.7 25.4 %spread.1 = (bf16[16,2048,256]{2,1,0:T(8,128)(2,1)}, bf16[16,2048,256]{2,1,0:T(8,128)(2,1)}, f32[16,256]{1,0:T(8,128)}, f32[16,256]{1,0:T(8,128)}, bf16[4,16,2048]{2,1,0:T(8,128)(2,1)}) custom-call(bf16[14,2048,256]{2,1,0:T(8,128)(2,1)} %get-tuple-element.23.a_ref, bf16[14,2048,256]{2,1,0:T(8,128)(2,1)} %get-tuple-element.24.b_ref, ...), custom_call_target="tpu_custom_call" | custom-call | bytes 58720256 | tf_op jit(solution)/shard_map/spread/pallas_call | solution.py:402
  707.1 12.7 %collective-permute-done.refs_2_ = bf16[2,2,512,256]{3,2,1,0:T(8,128)(2,1)S(1)} collective-permute-done((bf16[2,2,512,256]{3,2,1,0:T(8,128)(2,1)}, bf16[2,2,512,256]{3,2,1,0:T(8,128)(2,1)S(1)}, u32[]{:S(2)}, u32[]{:S(2)}) %collective-permute-start) | collective-permute-done | bytes 1048608 | tf_op jit(solution)/shard_map/ppermute | solution.py:485
  719.8 11.2 %collective-permute-done.1.refs_3_ = bf16[2,2,512,256]{3,2,1,0:T(8,128)(2,1)S(1)} collective-permute-done((bf16[2,2,512,256]{3,2,1,0:T(8,128)(2,1)}, bf16[2,2,512,256]{3,2,1,0:T(8,128)(2,1)S(1)}, u32[]{:S(2)}, u32[]{:S(2)}) %collective-permute-start.1) | collective-permute-done | bytes 1048608 | tf_op jit(solution)/shard_map/ppermute | solution.py:485
  731.0 1.3 join.2
  732.4 0.0 collective-permute-done.2.refs_2_
  732.4 1.0 join.3
Async XLA Ops:
  676.1 43.7 %collective-permute-start = (bf16[2,2,512,256]{3,2,1,0:T(8,128)(2,1)}, bf16[2,2,512,256]{3,2,1,0:T(8,128)(2,1)S(1)}, u32[]{:S(2)}, u32[]{:S(2)}) collective-permute-start(bf16[2,2,512,256]{3,2,1,0:T(8,128)(2,1)} %get-tuple-element.31), channel_id=1, source_target_pairs={{0,1},{1,2},{2,3},{3,0},{4,5},{5,6},{6,7},{7,4},{8,9},{9,10},{10,1... | collective-permute-start | bytes 3145736 | tf_op jit(solution)/shard_map/ppermute | solution.py:485
  676.2 54.9 %collective-permute-start.1 = (bf16[2,2,512,256]{3,2,1,0:T(8,128)(2,1)}, bf16[2,2,512,256]{3,2,1,0:T(8,128)(2,1)S(1)}, u32[]{:S(2)}, u32[]{:S(2)}) collective-permute-start(bf16[2,2,512,256]{3,2,1,0:T(8,128)(2,1)} %get-tuple-element.32), channel_id=1, source_target_pairs={{0,2},{1,3},{2,0},{3,1},{4,6},{5,7},{6,4},{7,5},{8,10},{9,11},{10,... | collective-permute-start | bytes 3145736 | tf_op jit(solution)/shard_map/ppermute | solution.py:485
  679.7 52.7 %collective-permute-start.2 = (bf16[2,2,512,256]{3,2,1,0:T(8,128)(2,1)}, bf16[2,2,512,256]{3,2,1,0:T(8,128)(2,1)S(1)}, u32[]{:S(2)}, u32[]{:S(2)}) collective-permute-start(bf16[2,2,512,256]{3,2,1,0:T(8,128)(2,1)} %get-tuple-element.35), channel_id=1, source_target_pairs={{0,3},{1,0},{2,1},{3,2},{4,7},{5,4},{6,5},{7,6},{8,11},{9,8},{10,9... | collective-permute-start | bytes 3145736 | tf_op jit(solution)/shard_map/ppermute | solution.py:485

commit v2 on v1

--- a/solution.py
+++ b/solution.py
@@ -181,19 +181,12 @@
         others("zero", me, n, lambda p: swap(m, e, me, p).start())
         if i == 1:
             others("zero", me, n, lambda p: row_copy(me, p).start())
-            refill()
-
-            @pl.when(lead)
-            def _():
-                for k in heads[:2]:
-                    arrived(*k)
-                    narrow(first.at[k], *k)
-                    send_all(*k)
-                    keep(*k)
+
+    refill()
 
     @pl.when(lead)
     def _():
-        for k in heads[2:]:
+        for k in heads:
             arrived(*k)
             narrow(first.at[k], *k)
             send_all(*k)
@@ -486,8 +479,8 @@
     ]
     og, ou, sg, su, rt = spread(n, og, ou, tails[0], sg, su, rt)
     if n > 2:
-        og, ou = join(n, tuple(range(1, n - 1)), og, ou, arrived[:-1])
-    og, ou = join(n, (n - 1,), og, ou, arrived[-1:])
+        og, ou = join(n, (1,), og, ou, arrived[:1])
+    og, ou = join(n, tuple(range(2, n)) or (1,), og, ou, arrived[1:] or arrived)
     return og, ou, sg, su, rt.reshape(banks * heads, depth * n).T
 
 

time: 734 us -> 732 us (level)
  transfers between devices with their start and end apart: 3 -> 3, of which waited for: 2 -> 3; matrix products, arithmetic and copies ran while one was open for 0% -> 0% of each run, Pallas kernels for 4% -> 4%
where the time goes in v2:
time: 732 us
  Pallas kernels  706 us (96%)
  waiting for transfers between devices  19.1 us (3%)
    pallas_call x1, Pallas kernels, local(): pl.pallas_call(functools.partial(kernel, n, banks), out_shape=(serve, ser...  679 us
    pallas_call x1, Pallas kernels, spread(): pl.pallas_call(functools.partial(copy_kernel, n), grid=(experts,), in_spe...  25.4 us
    ppermute x3, waiting for transfers between devices, local(): lax.ppermute(tails[d], 'zero', [(i, (i + d) % n) for i in range(n)])  19.1 us
  transfers between devices with their start and end apart: 3, of which 3 were waited for; matrix products, arithmetic and copies ran while one was open for 0% of the time, Pallas kernels for 4%

profile of v2, /device:TPU:8, one launch (start us, length us, event | category | flops | bytes accessed | tf_op | source)
XLA Modules:
  0.0 731.6 jit_solution(15078631903088936408)
XLA Ops:
  0.6 678.5 %shard_map.83 = (bf16[14,2048,256]{2,1,0:T(8,128)(2,1)}, bf16[14,2048,256]{2,1,0:T(8,128)(2,1)}, f32[16,256]{1,0:T(8,128)}, f32[16,256]{1,0:T(8,128)}, bf16[4,16...) custom-call(f32[16,512,1024]{2,1,0:T(8,128)} %wg_ref.1, ...), custom_call_target="tpu_custom_call" | custom-call | tf_op jit(solution)/shard_map/pallas_call | solution.py:453
  679.2 0.1 collective-permute-start
  679.3 3.5 collective-permute-start.1
  682.8 1.9 collective-permute-start.2
  684.8 25.4 %spread.1 = (bf16[16,2048,256]{2,1,0:T(8,128)(2,1)}, bf16[16,2048,256]{2,1,0:T(8,128)(2,1)}, f32[16,256]{1,0:T(8,128)}, f32[16,256]{1,0:T(8,128)}, bf16[4,16,2048]{2,1,0:T(8,128)(2,1)}) custom-call(bf16[14,2048,256]{2,1,0:T(8,128)(2,1)} %get-tuple-element.23.a_ref, bf16[14,2048,256]{2,1,0:T(8,128)(2,1)} %get-tuple-element.24.b_ref, ...), custom_call_target="tpu_custom_call" | custom-call | bytes 58720256 | tf_op jit(solution)/shard_map/spread/pallas_call | solution.py:395
  710.2 7.1 collective-permute-done.refs_2_
  717.2 1.0 join.2
  718.2 10.2 %collective-permute-done.1.refs_2_ = bf16[2,2,512,256]{3,2,1,0:T(8,128)(2,1)S(1)} collective-permute-done((bf16[2,2,512,256]{3,2,1,0:T(8,128)(2,1)}, bf16[2,2,512,256]{3,2,1,0:T(8,128)(2,1)S(1)}, u32[]{:S(2)}, u32[]{:S(2)}) %collective-permute-start.1) | collective-permute-done | bytes 1048608 | tf_op jit(solution)/shard_map/ppermute | solution.py:478
  728.5 1.8 collective-permute-done.2.refs_3_
  730.3 1.3 join.3
Async XLA Ops:
  679.2 38.1 %collective-permute-start = (bf16[2,2,512,256]{3,2,1,0:T(8,128)(2,1)}, bf16[2,2,512,256]{3,2,1,0:T(8,128)(2,1)S(1)}, u32[]{:S(2)}, u32[]{:S(2)}) collective-permute-start(bf16[2,2,512,256]{3,2,1,0:T(8,128)(2,1)} %get-tuple-element.31), channel_id=1, source_target_pairs={{0,1},{1,2},{2,3},{3,0},{4,5},{5,6},{6,7},{7,4},{8,9},{9,10},{10,1... | collective-permute-start | bytes 3145736 | tf_op jit(solution)/shard_map/ppermute | solution.py:478
  679.3 49.2 %collective-permute-start.1 = (bf16[2,2,512,256]{3,2,1,0:T(8,128)(2,1)}, bf16[2,2,512,256]{3,2,1,0:T(8,128)(2,1)S(1)}, u32[]{:S(2)}, u32[]{:S(2)}) collective-permute-start(bf16[2,2,512,256]{3,2,1,0:T(8,128)(2,1)} %get-tuple-element.34), channel_id=1, source_target_pairs={{0,2},{1,3},{2,0},{3,1},{4,6},{5,7},{6,4},{7,5},{8,10},{9,11},{10,... | collective-permute-start | bytes 3145736 | tf_op jit(solution)/shard_map/ppermute | solution.py:478
  682.8 47.5 %collective-permute-start.2 = (bf16[2,2,512,256]{3,2,1,0:T(8,128)(2,1)}, bf16[2,2,512,256]{3,2,1,0:T(8,128)(2,1)S(1)}, u32[]{:S(2)}, u32[]{:S(2)}) collective-permute-start(bf16[2,2,512,256]{3,2,1,0:T(8,128)(2,1)} %get-tuple-element.35), channel_id=1, source_target_pairs={{0,3},{1,0},{2,1},{3,2},{4,7},{5,4},{6,5},{7,6},{8,11},{9,8},{10,9... | collective-permute-start | bytes 3145736 | tf_op jit(solution)/shard_map/ppermute | solution.py:478

commit v3 on v2

--- a/solution.py
+++ b/solution.py
@@ -263,6 +263,12 @@
             def _():
                 give(i, p).wait_recv()
 
+    @pl.when(jnp.logical_not(lead))
+    def _():
+        for k in heads:
+            send_all(*k)
+            keep(*k)
+
     def put(m, d):
         return pltpu.make_async_copy(
             sendbuf.at[m, pl.ds(main, TAIL), lax.rem(me + d, n)], tails[d].at[m], tail_sem.at[d, m]
@@ -294,10 +300,6 @@
 
     @pl.when(jnp.logical_not(lead))
     def _():
-        for k in heads:
-            send_all(*k)
-            keep(*k)
-
         def near(e, carry):
             for m in range(2):
                 send_at(m, e, 1)

time: 732 us -> 732 us (level)
  waiting for transfers between devices: 19.1 us -> 55.4 us
  Pallas kernels: 706 us -> 670 us
    pallas_call x1, Pallas kernels: 679 us -> 642 us  [local(): pl.pallas_call(functools.partial(kernel, n, banks), out_shape=(serve, ser...]
    ppermute x3, waiting for transfers between devices: 19.1 us -> 55.4 us  [local(): lax.ppermute(tails[d], 'zero', [(i, (i + d) % n) for i in range(n)])]
where the time goes in v3:
time: 732 us
  Pallas kernels  670 us (92%)
  waiting for transfers between devices  55.4 us (8%)
    pallas_call x1, Pallas kernels, local(): pl.pallas_call(functools.partial(kernel, n, banks), out_shape=(serve, ser...  642 us
    ppermute x3, waiting for transfers between devices, local(): lax.ppermute(tails[d], 'zero', [(i, (i + d) % n) for i in range(n)])  55.4 us
    pallas_call x1, Pallas kernels, spread(): pl.pallas_call(functools.partial(copy_kernel, n), grid=(experts,), in_spe...  25.4 us
  transfers between devices with their start and end apart: 3, of which 3 were waited for; matrix products, arithmetic and copies ran while one was open for 0% of the time, Pallas kernels for 4%

profile of v3, /device:TPU:8, one launch (start us, length us, event | category | flops | bytes accessed | tf_op | source)
XLA Modules:
  0.0 731.5 jit_solution(15565525108470319803)
XLA Ops:
  0.6 642.1 %shard_map.83 = (bf16[14,2048,256]{2,1,0:T(8,128)(2,1)}, bf16[14,2048,256]{2,1,0:T(8,128)(2,1)}, f32[16,256]{1,0:T(8,128)}, f32[16,256]{1,0:T(8,128)}, bf16[4,16...) custom-call(f32[16,512,1024]{2,1,0:T(8,128)} %wg_ref.1, ...), custom_call_target="tpu_custom_call" | custom-call | tf_op jit(solution)/shard_map/pallas_call | solution.py:455
  642.8 0.1 collective-permute-start
  642.8 3.5 collective-permute-start.1
  646.4 1.9 collective-permute-start.2
  648.3 25.4 %spread.1 = (bf16[16,2048,256]{2,1,0:T(8,128)(2,1)}, bf16[16,2048,256]{2,1,0:T(8,128)(2,1)}, f32[16,256]{1,0:T(8,128)}, f32[16,256]{1,0:T(8,128)}, bf16[4,16,2048]{2,1,0:T(8,128)(2,1)}) custom-call(bf16[14,2048,256]{2,1,0:T(8,128)(2,1)} %get-tuple-element.23.a_ref, bf16[14,2048,256]{2,1,0:T(8,128)(2,1)} %get-tuple-element.24.b_ref, ...), custom_call_target="tpu_custom_call" | custom-call | bytes 58720256 | tf_op jit(solution)/shard_map/spread/pallas_call | solution.py:397
  673.7 37.9 %collective-permute-done.refs_2_ = bf16[2,2,512,256]{3,2,1,0:T(8,128)(2,1)S(1)} collective-permute-done((bf16[2,2,512,256]{3,2,1,0:T(8,128)(2,1)}, bf16[2,2,512,256]{3,2,1,0:T(8,128)(2,1)S(1)}, u32[]{:S(2)}, u32[]{:S(2)}) %collective-permute-start) | collective-permute-done | bytes 1048608 | tf_op jit(solution)/shard_map/ppermute | solution.py:480
  711.6 1.0 join.2
  712.6 15.9 %collective-permute-done.1.refs_2_ = bf16[2,2,512,256]{3,2,1,0:T(8,128)(2,1)S(1)} collective-permute-done((bf16[2,2,512,256]{3,2,1,0:T(8,128)(2,1)}, bf16[2,2,512,256]{3,2,1,0:T(8,128)(2,1)S(1)}, u32[]{:S(2)}, u32[]{:S(2)}) %collective-permute-start.1) | collective-permute-done | bytes 1048608 | tf_op jit(solution)/shard_map/ppermute | solution.py:480
  728.5 1.6 collective-permute-done.2.refs_3_
  730.2 1.3 join.3
Async XLA Ops:
  642.8 68.9 %collective-permute-start = (bf16[2,2,512,256]{3,2,1,0:T(8,128)(2,1)}, bf16[2,2,512,256]{3,2,1,0:T(8,128)(2,1)S(1)}, u32[]{:S(2)}, u32[]{:S(2)}) collective-permute-start(bf16[2,2,512,256]{3,2,1,0:T(8,128)(2,1)} %get-tuple-element.31), channel_id=1, source_target_pairs={{0,1},{1,2},{2,3},{3,0},{4,5},{5,6},{6,7},{7,4},{8,9},{9,10},{10,1... | collective-permute-start | bytes 3145736 | tf_op jit(solution)/shard_map/ppermute | solution.py:480
  642.8 85.7 %collective-permute-start.1 = (bf16[2,2,512,256]{3,2,1,0:T(8,128)(2,1)}, bf16[2,2,512,256]{3,2,1,0:T(8,128)(2,1)S(1)}, u32[]{:S(2)}, u32[]{:S(2)}) collective-permute-start(bf16[2,2,512,256]{3,2,1,0:T(8,128)(2,1)} %get-tuple-element.34), channel_id=1, source_target_pairs={{0,2},{1,3},{2,0},{3,1},{4,6},{5,7},{6,4},{7,5},{8,10},{9,11},{10,... | collective-permute-start | bytes 3145736 | tf_op jit(solution)/shard_map/ppermute | solution.py:480
  646.4 83.8 %collective-permute-start.2 = (bf16[2,2,512,256]{3,2,1,0:T(8,128)(2,1)}, bf16[2,2,512,256]{3,2,1,0:T(8,128)(2,1)S(1)}, u32[]{:S(2)}, u32[]{:S(2)}) collective-permute-start(bf16[2,2,512,256]{3,2,1,0:T(8,128)(2,1)} %get-tuple-element.35), channel_id=1, source_target_pairs={{0,3},{1,0},{2,1},{3,2},{4,7},{5,4},{6,5},{7,6},{8,11},{9,8},{10,9... | collective-permute-start | bytes 3145736 | tf_op jit(solution)/shard_map/ppermute | solution.py:480
